TPU v7x, 32 devices: a whole 2x2x4 slice. The times are simulated.
32 devices in a mesh: gx: 4 (over y, x), gy: 8 (over z, core).
Axes of the slice: x: 2, y: 2, z: 4, core: 2. Of those that a mesh axis runs over, the one named last changes fastest.
Arguments:
- traces: bfloat16 [8, 16, 128, 256], P('gx', 'gy'), may hold values from -6 to 6
- aperture: int32 [8, 16, 9], P('gx', 'gy'), may hold values 0 or 1
- geometry: int32 [8, 16, 3, 128], P('gx', 'gy'), may hold values from 0 to 63, as said below
- trace_weight: bfloat16 [8, 16, 128], P('gx', 'gy'), may hold values from 0.0087890625 to 0.03515625
- class_weight: float32 [14], replicated, may hold values from 0.3 to 1.5
- traveltime: int32 [14, 256], replicated, may hold values from 0 to 1114
Outputs:
- image: float32 [64, 64, 256], P('gx', 'gy')
Inputs may be any that keep to these rules, and one draw needn't show every extreme that they name: Row 0 of a trace's geometry is an inline midpoint among the 16 image columns of its block's tile, row 1 a crossline midpoint among its tile's 8 columns, row 2 an offset class below 8.
All inputs are finite; a program needn't handle non-finite values. No bound on the sum of `aperture` on one device may be relied on, other than what follows from the above.
Results may differ from a plain program's by a relative error of at most 0.0029.
Values may be sent and summed in bfloat16 or wider, within the bound.
A program may use at most 64 MiB of HBM per device.

v0:
```python
import functools

import jax
import jax.numpy as jnp
from jax import lax
from jax.experimental import pallas as pl
from jax.experimental.pallas import tpu as pltpu
from jax.sharding import PartitionSpec as P

PX = 16
PY = 8
DSTEP = 8
MESH = pl.DeviceIdType.MESH
BF = jnp.bfloat16
F32 = jnp.float32

ND = (2 * PX - 1 + 2 * PY - 1) // DSTEP + 1


def classes_at(dx, dy):
    far_x = 2 * PX - 1 if dx else PX - 1
    far_y = 2 * PY - 1 if dy else PY - 1
    return (far_x + far_y) // DSTEP + 1


def kernel(
    n_x, n_y, traces_at, geometry_at, weight_at, traveltime_at, aperture_at, class_weight_at,
    total, from_x, traces, geometry, weight, traveltime, aperture, class_weight,
    interp, taps, values, amplitude, own, y_out, y_in, x_out, x_in,
    load_sem, send_sem, recv_sem,
):
    loads = [
        pltpu.make_async_copy(src, dst, load_sem.at[n])
        for n, (src, dst) in enumerate(
            (
                (traveltime_at, traveltime), (traces_at, traces), (geometry_at, geometry),
                (weight_at, weight), (aperture_at, aperture), (class_weight_at, class_weight),
            )
        )
    ]
    for load in loads:
        load.start()
    bx, by, tr, ns = traces.shape
    nc, nt = traveltime.shape
    nj = bx * by * tr
    cols = PX * PY
    nh = nc - ND + 1
    me_x = lax.axis_index("gx")
    me_y = lax.axis_index("gy")
    turn = 2 * lax.rem(me_x, 2) - 1
    step_x = (turn, -turn)
    step_y = (-1, 1)
    has_x = [jnp.logical_and(me_x + s >= 0, me_x + s < n_x) for s in step_x]
    has_y = [me_y > 0, me_y < n_y - 1]
    barrier = pltpu.get_barrier_semaphore()
    for k in range(2):
        @pl.when(has_x[k])
        def _(k=k):
            pl.semaphore_signal(
                barrier, inc=1, device_id={"gx": me_x + step_x[k]}, device_id_type=MESH
            )

        @pl.when(has_y[k])
        def _(k=k):
            pl.semaphore_signal(
                barrier, inc=1, device_id={"gy": me_y + step_y[k]}, device_id_type=MESH
            )

    def copy(src, dst, number, device):
        return pltpu.make_async_remote_copy(
            src_ref=src, dst_ref=dst,
            send_sem=send_sem.at[number], recv_sem=recv_sem.at[number],
            device_id=device, device_id_type=MESH,
        )

    along_y = [
        [copy(y_out.at[n, k], y_in.at[n, k], 2 * n + k, {"gy": me_y + step_y[k]}) for k in range(2)]
        for n in range(3)
    ]
    along_x = [
        copy(x_out.at[k], x_in.at[k], 6 + k, {"gx": me_x + step_x[k]}) for k in range(2)
    ]

    def when(there, act):
        pl.when(there)(act)

    def send_y(n):
        for k in range(2):
            when(has_y[k], along_y[n][k].start)

    def arrive_y(n):
        for k in range(2):
            when(has_y[1 - k], along_y[n][k].wait_recv)

    for k in range(2):
        @pl.when(jnp.logical_not(has_y[1 - k]))
        def _(k=k):
            for n in range(3):
                y_in[n, k] = jnp.zeros(y_in.shape[2:], BF)

        @pl.when(jnp.logical_not(has_x[k]))
        def _(k=k):
            x_in[k] = jnp.zeros(x_in.shape[1:], BF)

    blocks = [(i, k) for i in range(bx) for k in range(by)]

    def row(ref, r):
        return jnp.concatenate([ref[i, r, k : k + 1, :] for i, k in blocks], axis=1)

    sample_ids = lax.broadcasted_iota(jnp.int32, (ns, nt), 0).astype(F32).astype(BF)
    zero = jnp.zeros((), BF)
    loads[0].wait()
    quarter = traveltime[...]
    first = (quarter >> 2).astype(F32)
    fraction = (quarter & 3).astype(F32) * 0.25
    first_b, next_b = first.astype(BF), (first + 1.0).astype(BF)
    frac_b, rest_b = fraction.astype(BF), (1.0 - fraction).astype(BF)
    for c in range(nc):
        interp[c] = jnp.where(
            sample_ids == first_b[c : c + 1, :],
            rest_b[c : c + 1, :],
            jnp.where(sample_ids == next_b[c : c + 1, :], frac_b[c : c + 1, :], zero),
        )

    for load in loads[1:]:
        load.wait()
    samples = traces[...].reshape(nj, ns)
    for c in range(nc):
        taps[c] = jnp.dot(samples, interp[c], preferred_element_type=F32).astype(BF)

    for b, (i, k) in enumerate(blocks):
        offset_row = geometry[i, 2, k : k + 1, :].astype(F32)
        offset_col = jnp.broadcast_to(offset_row, (tr, tr)).T.astype(BF)
        for r in range(0, tr, 16):
            rows = pl.ds(b * tr + r, 16)
            o = offset_col[r : r + 16, :]
            value = at_class = [
                [taps[c, rows, pl.ds(t, tr)] for t in range(0, nt, tr)] for c in range(nc)
            ]
            is_last = o == BF(nh - 1)
            bit = 1
            while 2 * bit < nh - 1:
                bit *= 2
            while bit:
                digit = o >= BF(bit)
                o = jnp.where(digit, o - BF(bit), o)
                value = [
                    [jnp.where(digit, high, low) for high, low in zip(value[c + bit], value[c])]
                    for c in range(ND + bit - 1)
                ]
                bit //= 2
            value[ND - 1] = [
                jnp.where(is_last, last, v) for last, v in zip(at_class[nc - 1], value[ND - 1])
            ]
            for d in range(ND):
                for n, v in enumerate(value[d]):
                    values[pl.ds(d * nj + b * tr + r, 16), pl.ds(n * tr, tr)] = v

    offset = row(geometry, 2)
    trace_weight = jnp.concatenate([weight[i, k : k + 1, :] for i, k in blocks], axis=1).astype(F32)
    scaled = []
    for d in range(ND):
        factor = jnp.zeros((1, nj), F32)
        for h in range(nh):
            factor = jnp.where(offset == h, class_weight[h + d], factor)
        scaled.append((trace_weight * factor).astype(BF).astype(F32))

    point = lax.broadcasted_iota(jnp.int32, (cols, nj), 0)
    point_x = (point // PY).astype(F32).astype(BF)
    point_y = (point % PY).astype(F32).astype(BF)
    mid_x = row(geometry, 0) - me_x * PX
    mid_y = row(geometry, 1) - me_y * PY
    grid = 136.0
    shift = (DSTEP - 1) / (2 * DSTEP)
    away_x = {
        dx: jnp.abs(point_x - (mid_x - at * PX).astype(F32).astype(BF)) * BF(1 / DSTEP)
        for dx, at in ((0, 0), (1, turn), (-1, -turn))
    }
    away_y = {
        dy: jnp.abs(point_y - (mid_y - dy * PY).astype(F32).astype(BF)) * BF(1 / DSTEP) - BF(shift)
        for dy in (-1, 0, 1)
    }

    def migrate(tiles):
        depth = classes_at(*tiles[0]) * nj
        for n, (dx, dy) in enumerate(tiles):
            level = (away_x[dx] + away_y[dy]) + BF(grid)
            entry = (dx * turn + 1) * 3 + (dy + 1)
            live = jnp.concatenate(
                [jnp.full((1, tr), aperture[i, k, entry], jnp.int32) for i, k in blocks], axis=1
            ).astype(F32)
            for d in range(classes_at(dx, dy)):
                amplitude[pl.ds(n * cols, cols), pl.ds(d * nj, nj)] = jnp.where(
                    level == BF(grid + d), (scaled[d] * live).astype(BF), zero
                )
        part = jnp.dot(
            amplitude[pl.ds(0, len(tiles) * cols), pl.ds(0, depth)],
            values[pl.ds(0, depth), :],
            preferred_element_type=F32,
        )
        return [part[n * cols : (n + 1) * cols] for n in range(len(tiles))]

    for n, dx in enumerate((1, -1, 0)):
        for k, part in enumerate(migrate([(dx, -1), (dx, 1)])):
            y_out[n, k] = part.astype(BF)
        if n == 0:
            there = [t.astype(jnp.int32) for t in has_x + has_y]
            pl.semaphore_wait(barrier, sum(there))
        send_y(n)
    for k, part in enumerate(migrate([(1, 0), (-1, 0)])):
        own[k] = part
    own[2] = migrate([(0, 0)])[0]

    def summed(n):
        arrive_y(n)
        return own[n] + y_in[n, 0].astype(F32) + y_in[n, 1].astype(F32)

    for k in range(2):
        x_out[k] = summed(k).astype(BF)
        when(has_x[k], along_x[k].start)
    total[...] = summed(2)
    for k in range(2):
        when(has_x[k], along_x[k].wait_recv)
        from_x[k] = x_in[k]
    for k in range(2):
        for n in range(3):
            when(has_y[k], along_y[n][k].wait_send)
        when(has_x[k], along_x[k].wait_send)


def per_device(n_x, n_y, traces, aperture, geometry, trace_weight, class_weight, traveltime):
    bx, by, tr, ns = traces.shape
    nc, nt = traveltime.shape
    nj = bx * by * tr
    cols = PX * PY
    geometry = jnp.transpose(geometry, (0, 2, 1, 3))
    vmem = pl.BlockSpec(memory_space=pltpu.VMEM)
    total, from_x = pl.pallas_call(
        functools.partial(kernel, n_x, n_y),
        out_shape=(pltpu.VMEM((cols, nt), F32), pltpu.VMEM((2, cols, nt), BF)),
        in_specs=[pl.BlockSpec(memory_space=pltpu.HBM)] * 6,
        out_specs=(vmem, vmem),
        scratch_shapes=[
            pltpu.VMEM(traces.shape, traces.dtype),
            pltpu.VMEM(geometry.shape, geometry.dtype),
            pltpu.VMEM(trace_weight.shape, trace_weight.dtype),
            pltpu.VMEM(traveltime.shape, traveltime.dtype),
            pltpu.SMEM(aperture.shape, aperture.dtype),
            pltpu.SMEM(class_weight.shape, class_weight.dtype),
            pltpu.VMEM((nc, ns, nt), BF),
            pltpu.VMEM((nc, nj, nt), BF),
            pltpu.VMEM((ND * nj, nt), BF),
            pltpu.VMEM((2 * cols, ND * nj), BF),
            pltpu.VMEM((3, cols, nt), F32),
            pltpu.VMEM((3, 2, cols, nt), BF),
            pltpu.VMEM((3, 2, cols, nt), BF),
            pltpu.VMEM((2, cols, nt), BF),
            pltpu.VMEM((2, cols, nt), BF),
            pltpu.SemaphoreType.DMA((6,)),
            pltpu.SemaphoreType.DMA((8,)),
            pltpu.SemaphoreType.DMA((8,)),
        ],
        compiler_params=pltpu.CompilerParams(collective_id=0, has_side_effects=True),
    )(traces, geometry, trace_weight, traveltime, aperture, class_weight)
    image = total + from_x[0].astype(F32) + from_x[1].astype(F32)
    return image.reshape(PX, PY, nt)


def solution(mesh):
    return jax.shard_map(
        functools.partial(per_device, mesh.shape["gx"], mesh.shape["gy"]),
        mesh=mesh,
        in_specs=(
            P("gx", "gy", None, None),
            P("gx", "gy", None),
            P("gx", "gy", None, None),
            P("gx", "gy", None),
            P(),
            P(),
        ),
        out_specs=P("gx", "gy", None),
        check_vma=False,
    )
```

profile of v0, /device:TPU:1, one launch (start us, length us, event | category | flops | bytes accessed | tf_op | source)
XLA Modules:
  0.0 13.7 jit_solution(2786372452938880969)
XLA Ops:
  0.0 13.0 %shard_map.64 = (f32[128,256]{1,0:T(8,128)S(1)}, bf16[2,128,256]{2,1,0:T(8,128)(2,1)S(1)}) custom-call(bf16[2,2,128,256]{3,2,1,0:T(8,128)(2,1)} %traces_at.1, s32[2,3,2,128]{3,2,1,0:T(2,128)} %bitcast.9, bf16[2,2,128]{2,1,0:T(2,128)(2,1)} %weight_at.1, s32[14,256]{1,0:T(8,128)} %traveltime_at.1, s32[2,2,9]{2,1,0:T(2,128)} %aperture_at.1, f32[14]{0:T(128)} %class_weight_at.1), custom_call_target="tpu_custom_call" | custom-call | tf_op jit(solution)/shard_map/pallas_call | solution.py:238
  13.0 0.7 %fusion = f32[16,8,256]{2,1,0:T(8,128)} fusion(f32[128,256]{1,0:T(8,128)S(1)} %get-tuple-element.7, bf16[2,128,256]{2,1,0:T(8,128)(2,1)S(1)} %get-tuple-element.8), kind=kLoop, calls=%fused_computation.1 | loop fusion | flops 131072 | bytes 393216 | tf_op jit(solution)/shard_map/reshape | solution.py:266
where the time goes:
time: 13.9 us; the launch traced here: 13.7 us
  Pallas kernels  13 us (94%)
  other arithmetic  0.68 us (5%)
    pallas_call x1, Pallas kernels, per_device(): pl.pallas_call(functools.partial(kernel, n_x, n_y), out_shape=(pltpu.VMEM...  13 us
    reshape x1, other arithmetic, per_device(): return image.reshape(PX, PY, nt)  0.68 us

commit v1 on v0

v1 whole, which is shorter than its diff:
```python
import functools

import jax
import jax.numpy as jnp
from jax import lax
from jax.experimental import pallas as pl
from jax.experimental.pallas import tpu as pltpu
from jax.sharding import PartitionSpec as P

PX = 16
PY = 8
DSTEP = 8
NH = 8
MESH = pl.DeviceIdType.MESH
BF = jnp.bfloat16
F32 = jnp.float32
ROWS = 16
GRID = 136.0
SHIFT = (DSTEP - 1) / (2 * DSTEP)

ND = (2 * PX - 1 + 2 * PY - 1) // DSTEP + 1
NCLASS = NH + ND - 1


def classes_at(dx, dy):
    far_x = 2 * PX - 1 if dx else PX - 1
    far_y = 2 * PY - 1 if dy else PY - 1
    return (far_x + far_y) // DSTEP + 1


def kernel(
    n_x, n_y, traces_at, geometry_at, weight_at, traveltime_at, aperture_at, class_weight_at,
    total, from_x, traces, geometry, weight, traveltime, aperture, class_weight,
    interp, digits, taps, values, amplitude, own, y_out, y_in, x_out, x_in,
    load_sem, send_sem, recv_sem,
):
    bx, by, tr, ns = traces.shape
    nt = traveltime.shape[1]
    nj = bx * by * tr
    cols = PX * PY
    blocks = [(i, k) for i in range(bx) for k in range(by)]
    pairs = [(traveltime_at, traveltime), (geometry_at, geometry), (weight_at, weight)]
    pairs += [(aperture_at, aperture), (class_weight_at, class_weight)]
    pairs += [(traces_at.at[i, k], traces.at[i, k]) for i, k in blocks]
    loads = [
        pltpu.make_async_copy(src, dst, load_sem.at[n]) for n, (src, dst) in enumerate(pairs)
    ]
    for load in loads:
        load.start()
    me_x = lax.axis_index("gx")
    me_y = lax.axis_index("gy")
    side = 2 * lax.rem(me_y, 2) - 1
    step_x = (-1, 1)
    step_y = (side, -side)
    has_x = [me_x > 0, me_x < n_x - 1]
    has_y = [jnp.logical_and(me_y + s >= 0, me_y + s < n_y) for s in step_y]
    barrier = pltpu.get_barrier_semaphore()

    def when(there, act):
        pl.when(there)(act)

    for k in range(2):
        @pl.when(has_x[k])
        def _(k=k):
            pl.semaphore_signal(
                barrier, inc=1, device_id={"gx": me_x + step_x[k]}, device_id_type=MESH
            )

        @pl.when(has_y[k])
        def _(k=k):
            pl.semaphore_signal(
                barrier, inc=1, device_id={"gy": me_y + step_y[k]}, device_id_type=MESH
            )

    def copy(src, dst, number, device):
        return pltpu.make_async_remote_copy(
            src_ref=src, dst_ref=dst,
            send_sem=send_sem.at[number], recv_sem=recv_sem.at[number],
            device_id=device, device_id_type=MESH,
        )

    along_y = [
        [copy(y_out.at[n, k], y_in.at[n, k], 2 * n + k, {"gy": me_y + step_y[k]}) for k in range(2)]
        for n in range(3)
    ]
    along_x = [
        copy(x_out.at[k], x_in.at[k], 6 + k, {"gx": me_x + step_x[k]}) for k in range(2)
    ]

    for k in range(2):
        @pl.when(jnp.logical_not(has_y[k]))
        def _(k=k):
            for n in range(3):
                y_in[n, k] = jnp.zeros(y_in.shape[2:], BF)

        @pl.when(jnp.logical_not(has_x[1 - k]))
        def _(k=k):
            x_in[k] = jnp.zeros(x_in.shape[1:], BF)

    groups = [blocks[b : b + by] for b in range(0, len(blocks), by)]
    zero = jnp.zeros((), BF)

    def spread(row):
        return jnp.broadcast_to(row, (ROWS, row.shape[1])).astype(BF)

    loads[0].wait()
    quarter = traveltime[...]
    first = (quarter >> 2).astype(F32)
    fraction = (quarter & 3).astype(F32) * 0.25
    row_ids = lax.broadcasted_iota(jnp.int32, (ROWS, nt), 0).astype(F32).astype(BF)

    def build_interp(c):
        at, part = first[c : c + 1, :], fraction[c : c + 1, :]
        at_b, next_b = spread(at), spread(at + 1.0)
        part_b, rest_b = spread(part), spread(1.0 - part)
        for r in range(0, ns, ROWS):
            ids = row_ids + BF(r)
            interp[c, pl.ds(r, ROWS), :] = jnp.where(
                ids == at_b, rest_b, jnp.where(ids == next_b, part_b, zero)
            )

    for c in range(NCLASS):
        build_interp(c)
    for load in loads[1:5]:
        load.wait()

    for b, (i, k) in enumerate(blocks):
        o = jnp.broadcast_to(geometry[i, 2, k : k + 1, :].astype(F32), (tr, tr)).T
        o = jnp.concatenate([o] * (nt // tr), axis=1).astype(BF)
        digits[pl.ds(b * tr, tr), :] = o

    def row_of(ref, r, group):
        return jnp.concatenate([ref[i, r, k : k + 1, :] for i, k in group], axis=1)

    def scaled(group, d):
        offset = row_of(geometry, 2, group)
        factor = jnp.zeros(offset.shape, F32)
        for h in range(NH):
            factor = jnp.where(offset == h, class_weight[h + d], factor)
        weights = jnp.concatenate([weight[i, k : k + 1, :] for i, k in group], axis=1).astype(F32)
        return (weights * factor).astype(BF).astype(F32)

    wide = by * tr
    scales = [[scaled(group, d) for d in range(ND)] for group in groups]
    row = lax.broadcasted_iota(jnp.int32, (ROWS, wide), 0)
    row_x = (row // PY).astype(F32).astype(BF)
    row_y = (row % PY).astype(F32).astype(BF)

    def build_amplitude(slot, dx, dy, nd, g):
        group = groups[g]
        mid_x = row_of(geometry, 0, group) - me_x * PX
        mid_y = row_of(geometry, 1, group) - me_y * PY
        at_x = row_x - spread((mid_x - dx * PX).astype(F32))
        away_y = jnp.abs(row_y - spread((mid_y - dy * PY).astype(F32)))
        away_y = away_y * BF(1 / DSTEP) - BF(SHIFT)
        entry = (dx + 1) * 3 + (dy + 1)
        live = jnp.concatenate(
            [jnp.full((1, tr), aperture[i, k, entry], jnp.int32) for i, k in group], axis=1
        ).astype(F32)
        scale = [spread(scales[g][d] * live) for d in range(nd)]
        for r in range(0, cols, ROWS):
            away_x = jnp.abs(at_x + BF(r // PY)) * BF(1 / DSTEP)
            level = (away_x + away_y) + BF(GRID)
            for d in range(nd):
                amplitude[slot, pl.ds(r, ROWS), pl.ds(d * nj + g * wide, wide)] = jnp.where(
                    level == BF(GRID + d), scale[d], zero
                )

    tiles = [(dx, dy) for dx in (-1, 1, 0) for dy in (side, -side)]
    tiles += [(dx, 0) for dx in (-1, 1, 0)]
    depths = [classes_at(dx, 1) for dx in (-1, 1, 0) for _ in range(2)]
    depths += [classes_at(dx, 0) for dx in (-1, 1, 0)]

    def amplitudes(slot):
        for g in range(len(groups)):
            build_amplitude(slot, *tiles[slot], depths[slot], g)

    def choose(r):
        rows = pl.ds(r, ROWS)
        o = digits[rows, :]
        now = [taps[c, rows, :] for c in range(NCLASS)]
        for bit in (4, 2, 1):
            take = o >= BF(bit)
            o = jnp.where(take, o - BF(bit), o)
            now = [jnp.where(take, now[c + bit], now[c]) for c in range(ND + bit - 1)]
        for d in range(ND):
            values[pl.ds(d * nj + r, ROWS), :] = now[d]

    def migrate(slot):
        total_part = None
        for g in range(len(groups)):
            left = jnp.concatenate(
                [
                    amplitude[slot, :, pl.ds(d * nj + g * wide, wide)]
                    for d in range(depths[slot])
                ],
                axis=1,
            )
            right = jnp.concatenate(
                [values[pl.ds(d * nj + g * wide, wide), :] for d in range(depths[slot])], axis=0
            )
            part = jnp.dot(left, right, preferred_element_type=F32)
            total_part = part if total_part is None else total_part + part
        return total_part

    amplitudes(0)
    for load in loads[5:]:
        load.wait()
    for g in range(len(groups)):
        for c in range(NCLASS):
            part = jnp.dot(
                traces[g].reshape(wide, ns), interp[c], preferred_element_type=F32
            )
            taps[c, pl.ds(g * wide, wide), :] = part.astype(BF)
            if g == 0 and c == 4:
                amplitudes(2)
            if g:
                count = wide // ROWS
                for r in range(c * count // NCLASS, (c + 1) * count // NCLASS):
                    choose((g - 1) * wide + r * ROWS)
    for r in range(wide // ROWS):
        choose((len(groups) - 1) * wide + r * ROWS)

    def send(n, k):
        when(has_y[k], along_y[n][k].start)

    def emit(n, k):
        y_out[n, k] = migrate(2 * n + k).astype(BF)

    emit(0, 0)
    amplitudes(1)
    there = [t.astype(jnp.int32) for t in has_x + has_y]
    pl.semaphore_wait(barrier, sum(there))
    send(0, 0)
    emit(1, 0)
    amplitudes(3)
    send(1, 0)
    emit(0, 1)
    emit(1, 1)
    amplitudes(4)
    amplitudes(5)
    send(0, 1)
    send(1, 1)
    emit(2, 0)
    emit(2, 1)
    for m in range(3):
        amplitudes(6 + m)
    send(2, 0)
    send(2, 1)
    for m in range(3):
        own[m] = migrate(6 + m)

    def summed(n):
        for k in range(2):
            when(has_y[k], along_y[n][k].wait_recv)
        return own[n] + y_in[n, 0].astype(F32) + y_in[n, 1].astype(F32)

    for k in range(2):
        x_out[k] = summed(k).astype(BF)
        when(has_x[k], along_x[k].start)
    total[...] = summed(2)
    for k in range(2):
        when(has_x[1 - k], along_x[k].wait_recv)
        from_x[k] = x_in[k]
    for k in range(2):
        for n in range(3):
            when(has_y[k], along_y[n][k].wait_send)
        when(has_x[k], along_x[k].wait_send)


def per_device(n_x, n_y, traces, aperture, geometry, trace_weight, class_weight, traveltime):
    bx, by, tr, ns = traces.shape
    nt = traveltime.shape[1]
    nj = bx * by * tr
    cols = PX * PY
    geometry = jnp.transpose(geometry, (0, 2, 1, 3))
    vmem = pl.BlockSpec(memory_space=pltpu.VMEM)
    total, from_x = pl.pallas_call(
        functools.partial(kernel, n_x, n_y),
        out_shape=(pltpu.VMEM((cols, nt), F32), pltpu.VMEM((2, cols, nt), BF)),
        in_specs=[pl.BlockSpec(memory_space=pltpu.HBM)] * 6,
        out_specs=(vmem, vmem),
        scratch_shapes=[
            pltpu.VMEM(traces.shape, traces.dtype),
            pltpu.VMEM(geometry.shape, geometry.dtype),
            pltpu.VMEM(trace_weight.shape, trace_weight.dtype),
            pltpu.VMEM(traveltime.shape, traveltime.dtype),
            pltpu.SMEM(aperture.shape, aperture.dtype),
            pltpu.SMEM(class_weight.shape, class_weight.dtype),
            pltpu.VMEM((NCLASS, ns, nt), BF),
            pltpu.VMEM((nj, nt), BF),
            pltpu.VMEM((NCLASS, nj, nt), BF),
            pltpu.VMEM((ND * nj, nt), BF),
            pltpu.VMEM((9, cols, ND * nj), BF),
            pltpu.VMEM((3, cols, nt), F32),
            pltpu.VMEM((3, 2, cols, nt), BF),
            pltpu.VMEM((3, 2, cols, nt), BF),
            pltpu.VMEM((2, cols, nt), BF),
            pltpu.VMEM((2, cols, nt), BF),
            pltpu.SemaphoreType.DMA((5 + bx * by,)),
            pltpu.SemaphoreType.DMA((8,)),
            pltpu.SemaphoreType.DMA((8,)),
        ],
        compiler_params=pltpu.CompilerParams(collective_id=0, has_side_effects=True),
    )(traces, geometry, trace_weight, traveltime, aperture, class_weight)
    image = total + from_x[0].astype(F32) + from_x[1].astype(F32)
    return image.reshape(PX, PY, nt)


def solution(mesh):
    return jax.shard_map(
        functools.partial(per_device, mesh.shape["gx"], mesh.shape["gy"]),
        mesh=mesh,
        in_specs=(
            P("gx", "gy", None, None),
            P("gx", "gy", None),
            P("gx", "gy", None, None),
            P("gx", "gy", None),
            P(),
            P(),
        ),
        out_specs=P("gx", "gy", None),
        check_vma=False,
    )
```

time: 13.9 us -> 12.7 us (0.914)
  Pallas kernels: 13 us -> 11.7 us
    pallas_call x1, Pallas kernels: 13 us -> 11.7 us  [per_device(): pl.pallas_call(functools.partial(kernel, n_x, n_y), out_shape=(pltpu.VMEM...]
where the time goes in v1:
time: 12.7 us; the launch traced here: 12.4 us
  Pallas kernels  11.7 us (92%)
  other arithmetic  0.68 us (5%)
    pallas_call x1, Pallas kernels, per_device(): pl.pallas_call(functools.partial(kernel, n_x, n_y), out_shape=(pltpu.VMEM...  11.7 us
    reshape x1, other arithmetic, per_device(): return image.reshape(PX, PY, nt)  0.68 us

profile of v1, /device:TPU:1, one launch (start us, length us, event | category | flops | bytes accessed | tf_op | source)
XLA Modules:
  0.0 12.4 jit_solution(2301271719542665981)
XLA Ops:
  0.0 11.7 %shard_map.64 = (f32[128,256]{1,0:T(8,128)S(1)}, bf16[2,128,256]{2,1,0:T(8,128)(2,1)S(1)}) custom-call(bf16[2,2,128,256]{3,2,1,0:T(8,128)(2,1)} %traces_at.1, s32[2,3,2,128]{3,2,1,0:T(2,128)} %bitcast.9, bf16[2,2,128]{2,1,0:T(2,128)(2,1)} %weight_at.1, s32[14,256]{1,0:T(8,128)} %traveltime_at.1, s32[2,2,9]{2,1,0:T(2,128)} %aperture_at.1, f32[14]{0:T(128)} %class_weight_at.1), custom_call_target="tpu_custom_call" | custom-call | tf_op jit(solution)/shard_map/pallas_call | solution.py:278
  11.8 0.7 %fusion = f32[16,8,256]{2,1,0:T(8,128)} fusion(f32[128,256]{1,0:T(8,128)S(1)} %get-tuple-element.7, bf16[2,128,256]{2,1,0:T(8,128)(2,1)S(1)} %get-tuple-element.8), kind=kLoop, calls=%fused_computation.1 | loop fusion | flops 131072 | bytes 393216 | tf_op jit(solution)/shard_map/reshape | solution.py:307

commit v2 on v1

--- a/solution.py
+++ b/solution.py
@@ -15,6 +15,7 @@
 BF = jnp.bfloat16
 F32 = jnp.float32
 ROWS = 16
+HALVES = 1
 GRID = 136.0
 SHIFT = (DSTEP - 1) / (2 * DSTEP)
 
@@ -79,12 +80,33 @@
             device_id=device, device_id_type=MESH,
         )
 
+    half = cols // HALVES
+
+    def part_of(h):
+        return pl.ds(h * half, half)
+
     along_y = [
-        [copy(y_out.at[n, k], y_in.at[n, k], 2 * n + k, {"gy": me_y + step_y[k]}) for k in range(2)]
+        [
+            [
+                copy(
+                    y_out.at[n, k, part_of(h)], y_in.at[n, k, part_of(h)],
+                    (2 * n + k) * HALVES + h, {"gy": me_y + step_y[k]},
+                )
+                for h in range(HALVES)
+            ]
+            for k in range(2)
+        ]
         for n in range(3)
     ]
     along_x = [
-        copy(x_out.at[k], x_in.at[k], 6 + k, {"gx": me_x + step_x[k]}) for k in range(2)
+        [
+            copy(
+                x_out.at[k, part_of(h)], x_in.at[k, part_of(h)],
+                (6 + k) * HALVES + h, {"gx": me_x + step_x[k]},
+            )
+            for h in range(HALVES)
+        ]
+        for k in range(2)
     ]
 
     for k in range(2):
@@ -121,13 +143,14 @@
 
     for c in range(NCLASS):
         build_interp(c)
-    for load in loads[1:5]:
+    for load in loads[1:]:
         load.wait()
 
-    for b, (i, k) in enumerate(blocks):
-        o = jnp.broadcast_to(geometry[i, 2, k : k + 1, :].astype(F32), (tr, tr)).T
-        o = jnp.concatenate([o] * (nt // tr), axis=1).astype(BF)
-        digits[pl.ds(b * tr, tr), :] = o
+    def build_digits():
+        for b, (i, k) in enumerate(blocks):
+            o = jnp.broadcast_to(geometry[i, 2, k : k + 1, :].astype(F32), (tr, tr)).T
+            o = jnp.concatenate([o] * (nt // tr), axis=1).astype(BF)
+            digits[pl.ds(b * tr, tr), :] = o
 
     def row_of(ref, r, group):
         return jnp.concatenate([ref[i, r, k : k + 1, :] for i, k in group], axis=1)
@@ -141,13 +164,13 @@
         return (weights * factor).astype(BF).astype(F32)
 
     wide = by * tr
-    scales = [[scaled(group, d) for d in range(ND)] for group in groups]
+    scales = []
     row = lax.broadcasted_iota(jnp.int32, (ROWS, wide), 0)
     row_x = (row // PY).astype(F32).astype(BF)
     row_y = (row % PY).astype(F32).astype(BF)
 
-    def build_amplitude(slot, dx, dy, nd, g):
-        group = groups[g]
+    def amplitude_pieces(slot, g):
+        (dx, dy), nd, group = tiles[slot], depths[slot], groups[g]
         mid_x = row_of(geometry, 0, group) - me_x * PX
         mid_y = row_of(geometry, 1, group) - me_y * PY
         at_x = row_x - spread((mid_x - dx * PX).astype(F32))
@@ -158,7 +181,8 @@
             [jnp.full((1, tr), aperture[i, k, entry], jnp.int32) for i, k in group], axis=1
         ).astype(F32)
         scale = [spread(scales[g][d] * live) for d in range(nd)]
-        for r in range(0, cols, ROWS):
+
+        def piece(r):
             away_x = jnp.abs(at_x + BF(r // PY)) * BF(1 / DSTEP)
             level = (away_x + away_y) + BF(GRID)
             for d in range(nd):
@@ -166,6 +190,8 @@
                     level == BF(GRID + d), scale[d], zero
                 )
 
+        return [functools.partial(piece, r) for r in range(0, cols, ROWS)]
+
     tiles = [(dx, dy) for dx in (-1, 1, 0) for dy in (side, -side)]
     tiles += [(dx, 0) for dx in (-1, 1, 0)]
     depths = [classes_at(dx, 1) for dx in (-1, 1, 0) for _ in range(2)]
@@ -173,7 +199,8 @@
 
     def amplitudes(slot):
         for g in range(len(groups)):
-            build_amplitude(slot, *tiles[slot], depths[slot], g)
+            for piece in amplitude_pieces(slot, g):
+                piece()
 
     def choose(r):
         rows = pl.ds(r, ROWS)
@@ -203,69 +230,81 @@
             total_part = part if total_part is None else total_part + part
         return total_part
 
-    amplitudes(0)
-    for load in loads[5:]:
-        load.wait()
+    steps = [range(c, min(c + 2, NCLASS)) for c in range(0, NCLASS, 2)]
     for g in range(len(groups)):
-        for c in range(NCLASS):
-            part = jnp.dot(
-                traces[g].reshape(wide, ns), interp[c], preferred_element_type=F32
-            )
-            taps[c, pl.ds(g * wide, wide), :] = part.astype(BF)
-            if g == 0 and c == 4:
-                amplitudes(2)
+        for n, classes in enumerate(steps):
+            right = jnp.concatenate([interp[c] for c in classes], axis=1)
+            part = jnp.dot(traces[g].reshape(wide, ns), right, preferred_element_type=F32)
+            for m, c in enumerate(classes):
+                taps[c, pl.ds(g * wide, wide), :] = part[:, m * nt : (m + 1) * nt].astype(BF)
+            if g == 0 and n == 0:
+                build_digits()
+            if g == 0 and n == 1:
+                scales.extend([scaled(group, d) for d in range(ND)] for group in groups)
+            if g == 0 and n >= 2:
+                whole = [p for q in range(len(groups)) for p in amplitude_pieces(0, q)] if n == 2 else whole
+                share = len(steps) - 2
+                for p in whole[(n - 2) * len(whole) // share : (n - 1) * len(whole) // share]:
+                    p()
             if g:
                 count = wide // ROWS
-                for r in range(c * count // NCLASS, (c + 1) * count // NCLASS):
+                for r in range(n * count // len(steps), (n + 1) * count // len(steps)):
                     choose((g - 1) * wide + r * ROWS)
     for r in range(wide // ROWS):
         choose((len(groups) - 1) * wide + r * ROWS)
 
     def send(n, k):
-        when(has_y[k], along_y[n][k].start)
+        for h in range(HALVES):
+            when(has_y[k], along_y[n][k][h].start)
 
     def emit(n, k):
         y_out[n, k] = migrate(2 * n + k).astype(BF)
 
     emit(0, 0)
-    amplitudes(1)
     there = [t.astype(jnp.int32) for t in has_x + has_y]
     pl.semaphore_wait(barrier, sum(there))
     send(0, 0)
+    amplitudes(2)
     emit(1, 0)
+    send(1, 0)
+    amplitudes(1)
     amplitudes(3)
-    send(1, 0)
     emit(0, 1)
     emit(1, 1)
+    send(0, 1)
+    send(1, 1)
     amplitudes(4)
     amplitudes(5)
-    send(0, 1)
-    send(1, 1)
     emit(2, 0)
     emit(2, 1)
-    for m in range(3):
-        amplitudes(6 + m)
     send(2, 0)
     send(2, 1)
     for m in range(3):
+        amplitudes(6 + m)
+    for m in range(3):
         own[m] = migrate(6 + m)
 
-    def summed(n):
+    def summed(n, h):
         for k in range(2):
-            when(has_y[k], along_y[n][k].wait_recv)
-        return own[n] + y_in[n, 0].astype(F32) + y_in[n, 1].astype(F32)
-
-    for k in range(2):
-        x_out[k] = summed(k).astype(BF)
-        when(has_x[k], along_x[k].start)
-    total[...] = summed(2)
-    for k in range(2):
-        when(has_x[1 - k], along_x[k].wait_recv)
-        from_x[k] = x_in[k]
-    for k in range(2):
-        for n in range(3):
-            when(has_y[k], along_y[n][k].wait_send)
-        when(has_x[k], along_x[k].wait_send)
+            when(has_y[k], along_y[n][k][h].wait_recv)
+        rows = part_of(h)
+        return own[n, rows] + y_in[n, 0, rows].astype(F32) + y_in[n, 1, rows].astype(F32)
+
+    for k in range(2):
+        for h in range(HALVES):
+            x_out[k, part_of(h)] = summed(k, h).astype(BF)
+            when(has_x[k], along_x[k][h].start)
+    for h in range(HALVES):
+        total[part_of(h), :] = summed(2, h)
+    for k in range(2):
+        for h in range(HALVES):
+            when(has_x[1 - k], along_x[k][h].wait_recv)
+            from_x[k, part_of(h)] = x_in[k, part_of(h)]
+    for k in range(2):
+        for h in range(HALVES):
+            for n in range(3):
+                when(has_y[k], along_y[n][k][h].wait_send)
+            when(has_x[k], along_x[k][h].wait_send)
 
 
 def per_device(n_x, n_y, traces, aperture, geometry, trace_weight, class_weight, traveltime):
@@ -298,8 +337,8 @@
             pltpu.VMEM((2, cols, nt), BF),
             pltpu.VMEM((2, cols, nt), BF),
             pltpu.SemaphoreType.DMA((5 + bx * by,)),
-            pltpu.SemaphoreType.DMA((8,)),
-            pltpu.SemaphoreType.DMA((8,)),
+            pltpu.SemaphoreType.DMA((8 * HALVES,)),
+            pltpu.SemaphoreType.DMA((8 * HALVES,)),
         ],
         compiler_params=pltpu.CompilerParams(collective_id=0, has_side_effects=True),
     )(traces, geometry, trace_weight, traveltime, aperture, class_weight)

time: 12.7 us -> 12.3 us (0.969)
  Pallas kernels: 11.7 us -> 11.3 us
    pallas_call x1, Pallas kernels: 11.7 us -> 11.3 us  [per_device(): pl.pallas_call(functools.partial(kernel, n_x, n_y), out_shape=(pltpu.VMEM...]
where the time goes in v2:
time: 12.3 us; the launch traced here: 12 us
  Pallas kernels  11.3 us (92%)
  other arithmetic  0.68 us (6%)
    pallas_call x1, Pallas kernels, per_device(): pl.pallas_call(functools.partial(kernel, n_x, n_y), out_shape=(pltpu.VMEM...  11.3 us
    reshape x1, other arithmetic, per_device(): return image.reshape(PX, PY, nt)  0.68 us

profile of v2, /device:TPU:1, one launch (start us, length us, event | category | flops | bytes accessed | tf_op | source)
XLA Modules:
  0.0 12.0 jit_solution(11539230175158077573)
XLA Ops:
  0.0 11.3 %shard_map.64 = (f32[128,256]{1,0:T(8,128)S(1)}, bf16[2,128,256]{2,1,0:T(8,128)(2,1)S(1)}) custom-call(bf16[2,2,128,256]{3,2,1,0:T(8,128)(2,1)} %traces_at.1, s32[2,3,2,128]{3,2,1,0:T(2,128)} %bitcast.9, bf16[2,2,128]{2,1,0:T(2,128)(2,1)} %weight_at.1, s32[14,256]{1,0:T(8,128)} %traveltime_at.1, s32[2,2,9]{2,1,0:T(2,128)} %aperture_at.1, f32[14]{0:T(128)} %class_weight_at.1), custom_call_target="tpu_custom_call" | custom-call | tf_op jit(solution)/shard_map/pallas_call | solution.py:317
  11.3 0.7 %fusion = f32[16,8,256]{2,1,0:T(8,128)} fusion(f32[128,256]{1,0:T(8,128)S(1)} %get-tuple-element.7, bf16[2,128,256]{2,1,0:T(8,128)(2,1)S(1)} %get-tuple-element.8), kind=kLoop, calls=%fused_computation.1 | loop fusion | flops 131072 | bytes 393216 | tf_op jit(solution)/shard_map/reshape | solution.py:346

commit v3 on v2

--- a/solution.py
+++ b/solution.py
@@ -32,7 +32,7 @@
 def kernel(
     n_x, n_y, traces_at, geometry_at, weight_at, traveltime_at, aperture_at, class_weight_at,
     total, from_x, traces, geometry, weight, traveltime, aperture, class_weight,
-    interp, digits, taps, values, amplitude, own, y_out, y_in, x_out, x_in,
+    interp, digits, taps, values, amplitude, own, y_out, y_in, x_out,
     load_sem, send_sem, recv_sem,
 ):
     bx, by, tr, ns = traces.shape
@@ -101,7 +101,7 @@
     along_x = [
         [
             copy(
-                x_out.at[k, part_of(h)], x_in.at[k, part_of(h)],
+                x_out.at[k, part_of(h)], from_x.at[k, part_of(h)],
                 (6 + k) * HALVES + h, {"gx": me_x + step_x[k]},
             )
             for h in range(HALVES)
@@ -117,7 +117,7 @@
 
         @pl.when(jnp.logical_not(has_x[1 - k]))
         def _(k=k):
-            x_in[k] = jnp.zeros(x_in.shape[1:], BF)
+            from_x[k] = jnp.zeros(from_x.shape[1:], BF)
 
     groups = [blocks[b : b + by] for b in range(0, len(blocks), by)]
     zero = jnp.zeros((), BF)
@@ -202,6 +202,9 @@
             for piece in amplitude_pieces(slot, g):
                 piece()
 
+    def keep(c, now):
+        taps[c] = now
+
     def choose(r):
         rows = pl.ds(r, ROWS)
         o = digits[rows, :]
@@ -231,27 +234,24 @@
         return total_part
 
     steps = [range(c, min(c + 2, NCLASS)) for c in range(0, NCLASS, 2)]
-    for g in range(len(groups)):
-        for n, classes in enumerate(steps):
-            right = jnp.concatenate([interp[c] for c in classes], axis=1)
-            part = jnp.dot(traces[g].reshape(wide, ns), right, preferred_element_type=F32)
-            for m, c in enumerate(classes):
-                taps[c, pl.ds(g * wide, wide), :] = part[:, m * nt : (m + 1) * nt].astype(BF)
-            if g == 0 and n == 0:
-                build_digits()
-            if g == 0 and n == 1:
-                scales.extend([scaled(group, d) for d in range(ND)] for group in groups)
-            if g == 0 and n >= 2:
-                whole = [p for q in range(len(groups)) for p in amplitude_pieces(0, q)] if n == 2 else whole
-                share = len(steps) - 2
-                for p in whole[(n - 2) * len(whole) // share : (n - 1) * len(whole) // share]:
-                    p()
-            if g:
-                count = wide // ROWS
-                for r in range(n * count // len(steps), (n + 1) * count // len(steps)):
-                    choose((g - 1) * wide + r * ROWS)
-    for r in range(wide // ROWS):
-        choose((len(groups) - 1) * wide + r * ROWS)
+    for n, classes in enumerate(steps):
+        right = jnp.concatenate([interp[c] for c in classes], axis=1)
+        part = jnp.dot(traces[...].reshape(nj, ns), right, preferred_element_type=F32)
+        for m, c in enumerate(classes):
+            now = part[:, m * nt : (m + 1) * nt].astype(BF)
+            keep(c, now)
+        if n == 0:
+            build_digits()
+        if n == 1:
+            scales.extend([scaled(group, d) for d in range(ND)] for group in groups)
+        if n == 2:
+            whole = [p for q in range(len(groups)) for p in amplitude_pieces(0, q)]
+        if n >= 2:
+            share = len(steps) - 2
+            for p in whole[(n - 2) * len(whole) // share : (n - 1) * len(whole) // share]:
+                p()
+    for r in range(0, nj, ROWS):
+        choose(r)
 
     def send(n, k):
         for h in range(HALVES):
@@ -299,7 +299,6 @@
     for k in range(2):
         for h in range(HALVES):
             when(has_x[1 - k], along_x[k][h].wait_recv)
-            from_x[k, part_of(h)] = x_in[k, part_of(h)]
     for k in range(2):
         for h in range(HALVES):
             for n in range(3):
@@ -335,7 +334,6 @@
             pltpu.VMEM((3, 2, cols, nt), BF),
             pltpu.VMEM((3, 2, cols, nt), BF),
             pltpu.VMEM((2, cols, nt), BF),
-            pltpu.VMEM((2, cols, nt), BF),
             pltpu.SemaphoreType.DMA((5 + bx * by,)),
             pltpu.SemaphoreType.DMA((8 * HALVES,)),
             pltpu.SemaphoreType.DMA((8 * HALVES,)),

time: 12.3 us -> 12.2 us (level)
  no operation moved by 1% of the time
where the time goes in v3:
time: 12.2 us; the launch traced here: 12 us
  Pallas kernels  11.3 us (93%)
  other arithmetic  0.68 us (6%)
    pallas_call x1, Pallas kernels, per_device(): pl.pallas_call(functools.partial(kernel, n_x, n_y), out_shape=(pltpu.VMEM...  11.3 us
    reshape x1, other arithmetic, per_device(): return image.reshape(PX, PY, nt)  0.68 us

profile of v3, /device:TPU:1, one launch (start us, length us, event | category | flops | bytes accessed | tf_op | source)
XLA Modules:
  0.0 12.0 jit_solution(271470850475079524)
XLA Ops:
  0.0 11.3 %shard_map.64 = (f32[128,256]{1,0:T(8,128)S(1)}, bf16[2,128,256]{2,1,0:T(8,128)(2,1)S(1)}) custom-call(bf16[2,2,128,256]{3,2,1,0:T(8,128)(2,1)} %traces_at.1, s32[2,3,2,128]{3,2,1,0:T(2,128)} %bitcast.9, bf16[2,2,128]{2,1,0:T(2,128)(2,1)} %weight_at.1, s32[14,256]{1,0:T(8,128)} %traveltime_at.1, s32[2,2,9]{2,1,0:T(2,128)} %aperture_at.1, f32[14]{0:T(128)} %class_weight_at.1), custom_call_target="tpu_custom_call" | custom-call | tf_op jit(solution)/shard_map/pallas_call | solution.py:316
  11.3 0.7 %fusion = f32[16,8,256]{2,1,0:T(8,128)} fusion(f32[128,256]{1,0:T(8,128)S(1)} %get-tuple-element.7, bf16[2,128,256]{2,1,0:T(8,128)(2,1)S(1)} %get-tuple-element.8), kind=kLoop, calls=%fused_computation.1 | loop fusion | flops 131072 | bytes 393216 | tf_op jit(solution)/shard_map/reshape | solution.py:344
